TPU v7x, 32 devices: a whole 2x2x4 slice. The times are simulated.
32 devices in a mesh: row: 4 (over y, x), col: 8 (over z, core).
Axes of the slice: x: 2, y: 2, z: 4, core: 2. Of those that a mesh axis runs over, the one named last changes fastest.
Arguments:
- coarse_left: float32 [32, 16384], P('col', 'row'), may hold values from -3 to 3
- coarse_right: float32 [32, 16384], P('row', 'col'), may hold values from -3 to 3
- stencil_left: int32 [65536], P('row'), may hold values from -1 to 16384, as said below
- weights_left: float32 [4, 65536], P(None, 'row'), may hold values from 0.1 to 0.6
- stencil_right: int32 [65536], P('col'), may hold values from -1 to 16384, as said below
- weights_right: float32 [4, 65536], P(None, 'col'), may hold values from 0.1 to 0.6
- tile_mask: int32 [16, 16], P('row', 'col'), may hold values 0 or 1
- sample_rows: int32 [16, 16, 2048], P('row', 'col'), may hold values from 0 to 4095
- sample_cols: int32 [16, 16, 2048], P('row', 'col'), may hold values from 0 to 4095
- sample_values: float32 [16, 16, 2048], P('row', 'col'), may hold values from -6 to 6
Outputs:
- left_new: float32 [32, 65536], P('col', 'row')
- right_new: float32 [32, 65536], P('row', 'col')
Inputs may be any that keep to these rules, and one draw needn't show every extreme that they name: stencil_left[i] is i // 4 - 1, i // 4 or i // 4 + 1. stencil_right[j] is j // 4 - 1, j // 4 or j // 4 + 1.
All inputs are finite; a program needn't handle non-finite values. No bound on the sum of `tile_mask` on one device may be relied on, other than what follows from the above.
Results may differ from a plain program's by a relative error of at most 0.0001.
Values sent between devices are 32-bit elements; how exact they have to be, the bound alone decides.
No kernel may reach another device: no remote copies, remote signals or barrier semaphores. Data moves between devices by JAX's collectives and lax.ppermute only.
A program may use at most 128 MiB of HBM per device.

v0:
```python
import functools

import jax
import jax.numpy as jnp
from jax import lax
from jax.experimental import pallas as pl
from jax.experimental.pallas import tpu as pltpu
from jax.sharding import PartitionSpec as P


TILES = 16
TILE = 4096
SPT = 2048
TAPS = 4
EDGE = 128
CHUNK = 256
BATCH = 1024


def split(values):
    high = values.astype(jnp.bfloat16)
    return high, (values - high.astype(jnp.float32)).astype(jnp.bfloat16)


def interpolate(padded, stencil, weights, keep, out, me, offset, tile, own_rank):
    rank = padded.shape[0]
    own = lax.broadcasted_iota(jnp.int32, (rank, 128), 0) // own_rank == me

    def group(g, _):
        column = pl.multiple_of(tile * TILE + g * 1024, 1024)
        start = pl.multiple_of(tile * (TILE // 4) + g * 256, 256)
        base = stencil[tile * (TILE // 1024) + g] + (EDGE - 1 - offset - start)
        window = padded[:, pl.ds(start, 512)]
        for u in range(8):
            low = (EDGE - 2 + 32 * u) // 64 * 64
            if EDGE + 35 + 32 * u > low + 128:
                low += 64
            part = window[:, low : low + 128]
            total = [None] * (rank // 8)
            for t in range(TAPS):
                at = jnp.broadcast_to(base[u : u + 1, :] + (t - low), (8, 128))
                weight = jnp.broadcast_to(weights[t : t + 1, pl.ds(column + 128 * u, 128)], (8, 128))
                for k in range(rank // 8):
                    taken = jnp.take_along_axis(
                        part[8 * k : 8 * k + 8], at, axis=1, mode="promise_in_bounds"
                    )
                    term = taken * weight
                    total[k] = term if total[k] is None else total[k] + term
            total = jnp.concatenate(total, axis=0)
            keep(g, u, total)
            out[:, pl.ds(column + 128 * u, 128)] = jnp.where(own, total, 0.0)
        return 0

    lax.fori_loop(0, TILE // 1024, group, 0)


def keep_split(table, tile):
    def keep(g, u, total):
        rank = total.shape[0]
        high, rest = split(total)
        to = pl.ds(pl.multiple_of((g * 4 + u // 2) * rank, rank), rank)
        lane = (u % 2) * 128
        table[tile, to, lane : lane + 128] = high
        table[tile, to, CHUNK + lane : CHUNK + lane + 128] = rest

    return keep


def keep_whole(table, tile):
    def keep(g, u, total):
        table[tile, :, pl.ds(pl.multiple_of(g * 1024 + u * 128, 128), 128)] = total

    return keep


def one_hot(index):
    lanes = lax.broadcasted_iota(jnp.int32, (CHUNK, index.shape[1]), 0)
    return jnp.where(lanes == (index & (CHUNK - 1)), 1.0, 0.0).astype(jnp.bfloat16)


def read(table, index, rank):
    hot = one_hot(index)
    found = jnp.dot(
        table, jnp.concatenate([hot, hot], axis=0), preferred_element_type=jnp.float32
    )
    chunk = jnp.broadcast_to(index >> 8, (rank, index.shape[1]))
    taken = found[:rank]
    for c in range(1, found.shape[0] // rank):
        taken = jnp.where(chunk == c, found[c * rank : (c + 1) * rank], taken)
    return taken


def read_lanes(table, index):
    rank, width = table.shape
    found = []
    for s in range(index.shape[1] // 128):
        at = jnp.broadcast_to(index[:, s * 128 : (s + 1) * 128], (8, 128))
        lane, chunk = at & 127, at >> 7
        taken = [None] * (rank // 8)
        for c in range(width // 128):
            for k in range(rank // 8):
                here = jnp.take_along_axis(
                    table[8 * k : 8 * k + 8, c * 128 : (c + 1) * 128],
                    lane,
                    axis=1,
                    mode="promise_in_bounds",
                )
                taken[k] = here if c == 0 else jnp.where(chunk == c, here, taken[k])
        found.append(jnp.concatenate(taken, axis=0))
    return jnp.concatenate(found, axis=1)


def add(out, values, index, tile):
    rank = values.shape[0]
    hot = one_hot(index)
    chunk = jnp.broadcast_to(index >> 8, values.shape)
    high, rest = split(values)
    zero = jnp.zeros(values.shape, jnp.bfloat16)
    left = jnp.concatenate(
        [
            jnp.concatenate(
                [jnp.where(chunk == c, high, zero), jnp.where(chunk == c, rest, zero)], axis=1
            )
            for c in range(TILE // CHUNK)
        ],
        axis=0,
    )
    summed = lax.dot_general(
        left,
        jnp.concatenate([hot, hot], axis=1),
        (((1,), (1,)), ((), ())),
        preferred_element_type=jnp.float32,
    )
    for c in range(TILE // CHUNK):
        at = pl.ds(pl.multiple_of(tile * TILE + c * CHUNK, CHUNK), CHUNK)
        out[:, at] += summed[c * rank : (c + 1) * rank]


def pad(low, main, high, out):
    out[:, :EDGE] = low[...]
    out[:, EDGE : EDGE + main.shape[1]] = main[...]
    out[:, EDGE + main.shape[1] :] = high[...]


def step(
    mask,
    left_low,
    left,
    left_high,
    right_low,
    right,
    right_high,
    stencil_left,
    weights_left,
    stencil_right,
    weights_right,
    rows,
    cols,
    values,
    left_parts,
    right_parts,
    left_padded,
    right_padded,
    left_table,
    right_table,
    left_out,
    right_out,
    even,
    odd,
    live,
    *,
    eta,
):
    rank = left.shape[0]
    tile_rows, tile_cols, samples = rows.shape
    me_row, me_col = lax.axis_index("row"), lax.axis_index("col")
    left_rank, right_rank = left_parts.shape[3], right_parts.shape[2]
    pad(left_low, left, left_high, left_padded)
    pad(right_low, right, right_high, right_padded)
    for a in range(tile_rows):
        interpolate(
            left_padded,
            stencil_left,
            weights_left,
            keep_split(left_table, a),
            left_out,
            me_col,
            me_row * left.shape[1],
            a,
            left_rank,
        )
    for b in range(tile_cols):
        interpolate(
            right_padded,
            stencil_right,
            weights_right,
            keep_whole(right_table, b),
            right_out,
            me_row,
            me_col * right.shape[1],
            b,
            right_rank,
        )

    count = jnp.int32(0)
    for tile in range(tile_rows * tile_cols):
        live[count] = tile
        count += (mask[tile // tile_cols, tile % tile_cols] != 0).astype(jnp.int32)
    held = (even, odd)
    batches = samples // BATCH
    even[...] = jnp.zeros_like(even)
    odd[...] = jnp.zeros_like(odd)

    def listed(array, tile, i):
        part = array[tile // tile_cols, :, i * BATCH : (i + 1) * BATCH]
        row = part[:1]
        for b in range(1, tile_cols):
            row = jnp.where(tile % tile_cols == b, part[b : b + 1], row)
        return row

    def errors(tile, i):
        a, b = tile // tile_cols, tile % tile_cols
        scale = mask[a, b].astype(jnp.float32) * (-eta)
        left_cols = read(left_table[a], listed(rows, tile, i), rank)
        right_cols = read_lanes(right_table.at[b], listed(cols, tile, i))
        product = jnp.sum(left_cols * right_cols, axis=0, keepdims=True)
        error = scale * (product - listed(values, tile, i))
        held[i % 2][0] = error * right_cols
        held[i % 2][1] = error * left_cols

    def adds(tile, i):
        add(left_out, held[i % 2][0], listed(rows, tile, i), tile // tile_cols)
        add(right_out, held[i % 2][1], listed(cols, tile, i), tile % tile_cols)

    def visit(n, _):
        tile, before = live[n], live[jnp.maximum(n - 1, 0)]
        for i in range(batches):
            if i:
                adds(tile, i - 1)
            else:
                adds(before, batches - 1)
            errors(tile, i)
        return 0

    lax.fori_loop(0, count, visit, 0)

    @pl.when(count > 0)
    def _():
        adds(live[count - 1], batches - 1)

    def left_group(i, _):
        half = left_parts.shape[4]
        for h in range(2):
            at = pl.multiple_of(i * 512, 512)
            part = left_out[:, pl.ds(h * half + at, 512)]
            for c in range(rank // left_rank):
                left_parts[h, (c % 2) ^ (me_col % 2), (c // 2) ^ (me_col // 2), :, pl.ds(at, 512)] = (
                    part[c * left_rank : (c + 1) * left_rank]
                )
        return 0

    def right_group(i, _):
        half = right_parts.shape[3]
        for h in range(2):
            at = pl.multiple_of(i * 512, 512)
            part = right_out[:, pl.ds(h * half + at, 512)]
            for r in range(rank // right_rank):
                right_parts[h, r ^ me_row, :, pl.ds(at, 512)] = part[
                    r * right_rank : (r + 1) * right_rank
                ]
        return 0

    lax.fori_loop(0, left_parts.shape[4] // 512, left_group, 0)
    lax.fori_loop(0, right_parts.shape[3] // 512, right_group, 0)


def swap(x, axis, distance):
    return lax.ppermute(x, axis, [(i, i ^ distance) for i in range(lax.axis_size(axis))])


def from_neighbours(x, axis):
    count = lax.axis_size(axis)
    forward = [(i, i + 1) for i in range(count - 1)]
    backward = [(target, source) for source, target in forward]
    low = lax.ppermute(x[:, x.shape[1] - EDGE :], axis, forward)
    high = lax.ppermute(x[:, :EDGE], axis, backward)
    return low, high


def put(buffer, x, index, axis=0):
    return lax.dynamic_update_index_in_dim(buffer, x, index, axis)


def gather(x, axis, me, count, unit):
    out = put(jnp.zeros((count,) + x.shape, x.dtype), x, me)
    for j in range(1, count):
        out = put(out, swap(x, axis, j * unit), me ^ j)
    return out


def halve(parts, axis, distances):
    parts = {j: parts[j] for j in range(parts.shape[0])}
    for step in distances:
        kept = [j for j in parts if not j & step]
        sent = jnp.stack([parts[j ^ step] for j in kept])
        came = swap(sent, axis[0], step * axis[1])
        parts = {j: parts[j] + came[i] for i, j in enumerate(kept)}
    return parts[0]


def on_device(
    coarse_left,
    coarse_right,
    stencil_left,
    weights_left,
    stencil_right,
    weights_right,
    tile_mask,
    sample_rows,
    sample_cols,
    sample_values,
):
    row, col = lax.axis_index("row"), lax.axis_index("col")
    rows, cols = lax.axis_size("row"), lax.axis_size("col")
    left_rank, left_width = coarse_left.shape
    right_rank, right_width = coarse_right.shape
    rank = left_rank * cols
    half = gather(coarse_left, "col", col // 2, cols // 2, 2)
    right = gather(coarse_right, "row", row, rows, 1).reshape(rank, right_width)
    right_low, right_high = from_neighbours(right, "col")
    other = swap(half, "col", 1)
    left = jnp.zeros((cols // 2, 2, left_rank, left_width), jnp.float32)
    left = put(put(left, half, col % 2, 1), other, 1 - col % 2, 1).reshape(rank, left_width)
    left_low, left_high = from_neighbours(left, "row")
    tile_rows, tile_cols, _ = sample_rows.shape
    smem = pl.BlockSpec(memory_space=pltpu.SMEM)
    vmem = pl.BlockSpec(memory_space=pltpu.VMEM)
    left_parts, right_parts = pl.pallas_call(
        functools.partial(step, eta=4.0 * TILE / (SPT * TILES)),
        out_shape=(
            jax.ShapeDtypeStruct((2, 2, cols // 2, left_rank, tile_rows * TILE // 2), jnp.float32),
            jax.ShapeDtypeStruct((2, rows, right_rank, tile_cols * TILE // 2), jnp.float32),
        ),
        in_specs=[smem] + [vmem] * 13,
        out_specs=(vmem, vmem),
        scratch_shapes=[
            pltpu.VMEM((rank, left_width + 2 * EDGE), jnp.float32),
            pltpu.VMEM((rank, right_width + 2 * EDGE), jnp.float32),
            pltpu.VMEM((tile_rows, TILE // CHUNK * rank, 2 * CHUNK), jnp.bfloat16),
            pltpu.VMEM((tile_cols, rank, TILE), jnp.float32),
            pltpu.VMEM((rank, tile_rows * TILE), jnp.float32),
            pltpu.VMEM((rank, tile_cols * TILE), jnp.float32),
            pltpu.VMEM((2, rank, BATCH), jnp.float32),
            pltpu.VMEM((2, rank, BATCH), jnp.float32),
            pltpu.SMEM((tile_rows * tile_cols + 1,), jnp.int32),
        ],
        compiler_params=pltpu.CompilerParams(vmem_limit_bytes=60 * 1024 * 1024),
    )(
        tile_mask,
        left_low,
        left,
        left_high,
        right_low,
        right,
        right_high,
        stencil_left.reshape(-1, 8, 128),
        weights_left,
        stencil_right.reshape(-1, 8, 128),
        weights_right,
        sample_rows,
        sample_cols,
        sample_values,
    )
    came = swap(left_parts[:, 1], "col", 1)
    left_added, right_parts = lax.optimization_barrier((left_parts[:, 0] + came, right_parts))
    left_sums, right_sums = [], []
    for h in range(2):
        turned = slice(None, None, 1 - 2 * h)
        left_sums.append(halve(left_added[h], ("col", 2), bits(cols // 2)[turned]))
        right_sums.append(halve(right_parts[h], ("row", 1), bits(rows)[turned]))
    return (jnp.concatenate(left_sums, axis=1), jnp.concatenate(right_sums, axis=1))


def bits(count):
    out = []
    while count > 1:
        count //= 2
        out.append(count)
    return out[::-1]


def solution(mesh):
    in_specs = (
        P("col", "row"),
        P("row", "col"),
        P("row"),
        P(None, "row"),
        P("col"),
        P(None, "col"),
        P("row", "col"),
        P("row", "col", None),
        P("row", "col", None),
        P("row", "col", None),
    )
    out_specs = (P("col", "row"), P("row", "col"))

    return jax.shard_map(
        on_device, mesh=mesh, in_specs=in_specs, out_specs=out_specs, check_vma=False
    )
```

profile of v0, /device:TPU:0, one launch (start us, length us, event | category | flops | bytes accessed | tf_op | source)
XLA Modules:
  0.0 103.8 jit_solution(6612471438325350714)
XLA Ops:
  0.6 3.1 %collective-permute-start = (f32[4,4096]{1,0:T(4,128)}, f32[4,4096]{1,0:T(4,128)S(1)}, u32[]{:S(2)}, u32[]{:S(2)}) collective-permute-start(f32[4,4096]{1,0:T(4,128)} %param.10), channel_id=1, source_target_pairs={{0,2},{1,3},{2,0},{3,1},{4,6},{5,7},{6,4},{7,5},{8,10},{9,11},{10,... | collective-permute-start | bytes 196616 | tf_op jit(solution)/shard_map/ppermute | solution.py:278
  3.7 2.5 %collective-permute-start.2 = (f32[4,4096]{1,0:T(4,128)}, f32[4,4096]{1,0:T(4,128)S(1)}, u32[]{:S(2)}, u32[]{:S(2)}) collective-permute-start(f32[4,4096]{1,0:T(4,128)} %param.10), channel_id=1, source_target_pairs={{0,6},{1,7},{2,4},{3,5},{4,2},{5,3},{6,0},{7,1},{8,14},{9,15},{10,... | collective-permute-start | bytes 196616 | tf_op jit(solution)/shard_map/ppermute | solution.py:278
  6.3 1.5 %collective-permute-start.6 = (f32[8,2048]{1,0:T(8,128)}, f32[8,2048]{1,0:T(8,128)S(1)}, u32[]{:S(2)}, u32[]{:S(2)}) collective-permute-start(f32[8,2048]{1,0:T(8,128)} %param.11), channel_id=1, source_target_pairs={{0,8},{8,0},{16,24},{24,16},{1,9},{9,1},{17,25},{25,17},{2,10},{10... | collective-permute-start | bytes 196616 | tf_op jit(solution)/shard_map/ppermute | solution.py:278
  7.8 1.5 %collective-permute-start.8 = (f32[8,2048]{1,0:T(8,128)}, f32[8,2048]{1,0:T(8,128)S(1)}, u32[]{:S(2)}, u32[]{:S(2)}) collective-permute-start(f32[8,2048]{1,0:T(8,128)} %param.11), channel_id=1, source_target_pairs={{0,24},{8,16},{16,8},{24,0},{1,25},{9,17},{17,9},{25,1},{2,26},{10... | collective-permute-start | bytes 196616 | tf_op jit(solution)/shard_map/ppermute | solution.py:278
  9.4 0.9 bitcast_dynamic-update-slice_fusion.9
  10.3 0.9 bitcast_dynamic-update-slice_fusion.5
  11.1 1.4 %collective-permute-start.7 = (f32[8,2048]{1,0:T(8,128)}, f32[8,2048]{1,0:T(8,128)S(1)}, u32[]{:S(2)}, u32[]{:S(2)}) collective-permute-start(f32[8,2048]{1,0:T(8,128)} %param.11), channel_id=1, source_target_pairs={{0,16},{8,24},{16,0},{24,8},{1,17},{9,25},{17,1},{25,9},{2,18},{10... | collective-permute-start | bytes 196616 | tf_op jit(solution)/shard_map/ppermute | solution.py:278
  12.5 3.1 %collective-permute-done.7 = f32[8,2048]{1,0:T(8,128)S(1)} collective-permute-done((f32[8,2048]{1,0:T(8,128)}, f32[8,2048]{1,0:T(8,128)S(1)}, u32[]{:S(2)}, u32[]{:S(2)}) %collective-permute-start.7) | collective-permute-done | bytes 65568 | tf_op jit(solution)/shard_map/ppermute | solution.py:278
  15.7 1.3 %collective-permute-start.10 = (f32[32,128]{1,0:T(8,128)S(1)}, f32[32,128]{1,0:T(8,128)S(1)}, u32[]{:S(2)}, u32[]{:S(2)}) collective-permute-start(f32[32,128]{1,0:T(8,128)S(1)} %get-tuple-element.28), channel_id=1, source_target_pairs={{1,0},{2,1},{3,2},{4,3},{5,4},{6,5},{7,6},{9,8},{10,9},{11,10},{12... | collective-permute-start | bytes 49160 | tf_op jit(solution)/shard_map/ppermute | solution.py:286
  17.0 3.0 %collective-permute-start.9 = (f32[32,128]{1,0:T(8,128)S(1)}, f32[32,128]{1,0:T(8,128)S(1)}, u32[]{:S(2)}, u32[]{:S(2)}) collective-permute-start(f32[32,128]{1,0:T(8,128)S(1)} %get-tuple-element.29), channel_id=1, source_target_pairs={{0,1},{1,2},{2,3},{3,4},{4,5},{5,6},{6,7},{8,9},{9,10},{10,11},{11... | collective-permute-start | bytes 49160 | tf_op jit(solution)/shard_map/ppermute | solution.py:285
  20.2 1.6 %collective-permute-start.3 = (f32[4,4,4096]{2,1,0:T(4,128)S(1)}, f32[4,4,4096]{2,1,0:T(4,128)S(1)}, u32[]{:S(2)}, u32[]{:S(2)}) collective-permute-start(f32[4,4,4096]{2,1,0:T(4,128)S(1)} %bitcast_dynamic-update-slice_fusion.6), channel_id=1, source_target_pairs={{0,1},{1,0},{2,3},{3,2},{4,5},{5,4},{6,7},{7,6},{8,9},{9,8},{10,11... | collective-permute-start | bytes 786440 | tf_op jit(solution)/shard_map/ppermute | solution.py:278
  21.9 1.0 %collective-permute-done.3 = f32[4,4,4096]{2,1,0:T(4,128)S(1)} collective-permute-done((f32[4,4,4096]{2,1,0:T(4,128)S(1)}, f32[4,4,4096]{2,1,0:T(4,128)S(1)}, u32[]{:S(2)}, u32[]{:S(2)}) %collective-permute-start.3) | collective-permute-done | bytes 262176 | tf_op jit(solution)/shard_map/ppermute | solution.py:278
  23.2 1.3 %collective-permute-start.5 = (f32[32,128]{1,0:T(8,128)S(1)}, f32[32,128]{1,0:T(8,128)S(1)}, u32[]{:S(2)}, u32[]{:S(2)}) collective-permute-start(f32[32,128]{1,0:T(8,128)S(1)} %get-tuple-element.26), channel_id=1, source_target_pairs={{8,0},{16,8},{24,16},{9,1},{17,9},{25,17},{10,2},{18,10},{26,18},{... | collective-permute-start | bytes 49160 | tf_op jit(solution)/shard_map/ppermute | solution.py:286
  24.5 4.5 %collective-permute-start.4 = (f32[32,128]{1,0:T(8,128)S(1)}, f32[32,128]{1,0:T(8,128)S(1)}, u32[]{:S(2)}, u32[]{:S(2)}) collective-permute-start(f32[32,128]{1,0:T(8,128)S(1)} %get-tuple-element.27), channel_id=1, source_target_pairs={{0,8},{8,16},{16,24},{1,9},{9,17},{17,25},{2,10},{10,18},{18,26},{... | collective-permute-start | bytes 49160 | tf_op jit(solution)/shard_map/ppermute | solution.py:285
  29.1 0.7 copy.13.mask
  29.8 0.7 collective-permute-done.4.left_low
  30.5 0.6 copy-done.7
  31.1 26.4 %shard_map.113 = (f32[2,2,4,4,8192]{4,3,2,1,0:T(4,128)}, f32[2,4,8,4096]{3,2,1,0:T(8,128)}) custom-call(s32[4,2]{1,0:T(4,128)} %copy.13.mask, f32[32,128]{1,0:T(8,128)} %copy-done.7, f32[32,4096]{1,0:T(8,128)} %copy-done, f32[32,128]{1,0:T(8,128)} %copy-done.6, f32[32,128]{1,0:T(8,128)} %copy-done.5, f32[32,2048]{1,0:T(8,128)} %bitcast.96, ...), custom_call_target="tpu_custom_call" | custom-call | tf_op jit(solution)/shard_map/pallas_call | solution.py:338
  57.5 1.4 %slice_bitcast_fusion.1 = f32[2,4,4,8192]{3,2,1,0:T(4,128)S(1)} fusion(f32[2,2,4,4,8192]{4,3,2,1,0:T(4,128)} %get-tuple-element.6), kind=kLoop, calls=%fused_computation.2 | loop fusion | bytes 2097152 | tf_op jit(solution)/shard_map/squeeze | solution.py:374
  59.0 6.9 %collective-permute-start.11 = (f32[2,4,4,8192]{3,2,1,0:T(4,128)S(1)}, f32[2,4,4,8192]{3,2,1,0:T(4,128)S(1)}, u32[]{:S(2)}, u32[]{:S(2)}) collective-permute-start(f32[2,4,4,8192]{3,2,1,0:T(4,128)S(1)} %slice_bitcast_fusion.1), channel_id=1, source_target_pairs={{0,1},{1,0},{2,3},{3,2},{4,5},{5,4},{6,7},{7,6},{8,9},{9,8},{10,11... | collective-permute-start | bytes 3145736 | tf_op jit(solution)/shard_map/ppermute | solution.py:278
  65.8 2.3 %collective-permute-done.11 = f32[2,4,4,8192]{3,2,1,0:T(4,128)S(1)} collective-permute-done((f32[2,4,4,8192]{3,2,1,0:T(4,128)S(1)}, f32[2,4,4,8192]{3,2,1,0:T(4,128)S(1)}, u32[]{:S(2)}, u32[]{:S(2)}) %collective-permute-start.11) | collective-permute-done | bytes 1048608 | tf_op jit(solution)/shard_map/ppermute | solution.py:278
  68.5 6.7 %collective-permute-start.14 = (f32[2,4,8192]{2,1,0:T(4,128)S(1)}, f32[2,4,8192]{2,1,0:T(4,128)S(1)}, u32[]{:S(2)}, u32[]{:S(2)}) collective-permute-start(f32[2,4,8192]{2,1,0:T(4,128)S(1)} %pad_maximum_fusion.1), channel_id=1, source_target_pairs={{0,4},{1,5},{2,6},{3,7},{4,0},{5,1},{6,2},{7,3},{8,12},{9,13},{10,... | collective-permute-start | bytes 786440 | tf_op jit(solution)/shard_map/ppermute | solution.py:278
  75.5 8.5 %collective-permute-start.18 = (f32[2,8,4096]{2,1,0:T(8,128)S(1)}, f32[2,8,4096]{2,1,0:T(8,128)S(1)}, u32[]{:S(2)}, u32[]{:S(2)}) collective-permute-start(f32[2,8,4096]{2,1,0:T(8,128)S(1)} %pad_maximum_fusion.4), channel_id=1, source_target_pairs={{0,16},{8,24},{16,0},{24,8},{1,17},{9,25},{17,1},{25,9},{2,18},{10... | collective-permute-start | bytes 786440 | tf_op jit(solution)/shard_map/ppermute | solution.py:278
  84.0 0.7 collective-permute-done.14
  84.8 4.2 %collective-permute-done.12 = f32[2,4,8192]{2,1,0:T(4,128)S(1)} collective-permute-done((f32[2,4,8192]{2,1,0:T(4,128)S(1)}, f32[2,4,8192]{2,1,0:T(4,128)S(1)}, u32[]{:S(2)}, u32[]{:S(2)}) %collective-permute-start.12) | collective-permute-done | bytes 262176 | tf_op jit(solution)/shard_map/ppermute | solution.py:278
  89.4 0.6 collective-permute-done.18
  90.0 1.5 %collective-permute-done.16 = f32[2,8,4096]{2,1,0:T(8,128)S(1)} collective-permute-done((f32[2,8,4096]{2,1,0:T(8,128)S(1)}, f32[2,8,4096]{2,1,0:T(8,128)S(1)}, u32[]{:S(2)}, u32[]{:S(2)}) %collective-permute-start.16) | collective-permute-done | bytes 262176 | tf_op jit(solution)/shard_map/ppermute | solution.py:278
  91.6 6.5 %collective-permute-start.17 = (f32[1,8,4096]{2,1,0:T(8,128)S(1)}, f32[1,8,4096]{2,1,0:T(8,128)S(1)}, u32[]{:S(2)}, u32[]{:S(2)}) collective-permute-start(f32[1,8,4096]{2,1,0:T(8,128)S(1)} %get-tuple-element.12), channel_id=1, source_target_pairs={{0,16},{8,24},{16,0},{24,8},{1,17},{9,25},{17,1},{25,9},{2,18},{10... | collective-permute-start | bytes 393224 | tf_op jit(solution)/shard_map/ppermute | solution.py:278
  98.2 0.8 pad_maximum_fusion.2
  98.9 2.1 %collective-permute-done.17 = f32[1,8,4096]{2,1,0:T(8,128)S(1)} collective-permute-done((f32[1,8,4096]{2,1,0:T(8,128)S(1)}, f32[1,8,4096]{2,1,0:T(8,128)S(1)}, u32[]{:S(2)}, u32[]{:S(2)}) %collective-permute-start.17) | collective-permute-done | bytes 131104 | tf_op jit(solution)/shard_map/ppermute | solution.py:278
  101.0 2.0 %collective-permute-done.19 = f32[1,8,4096]{2,1,0:T(8,128)S(1)} collective-permute-done((f32[1,8,4096]{2,1,0:T(8,128)S(1)}, f32[1,8,4096]{2,1,0:T(8,128)S(1)}, u32[]{:S(2)}, u32[]{:S(2)}) %collective-permute-start.19) | collective-permute-done | bytes 131104 | tf_op jit(solution)/shard_map/ppermute | solution.py:278
  103.0 0.7 pad_maximum_fusion.5
  (58 shorter events, 1.9 us)
Async XLA Ops:
  0.6 19.4 %collective-permute-start = (f32[4,4096]{1,0:T(4,128)}, f32[4,4096]{1,0:T(4,128)S(1)}, u32[]{:S(2)}, u32[]{:S(2)}) collective-permute-start(f32[4,4096]{1,0:T(4,128)} %param.10), channel_id=1, source_target_pairs={{0,2},{1,3},{2,0},{3,1},{4,6},{5,7},{6,4},{7,5},{8,10},{9,11},{10,... | collective-permute-start | bytes 196616 | tf_op jit(solution)/shard_map/ppermute | solution.py:278
  3.7 16.4 %collective-permute-start.2 = (f32[4,4096]{1,0:T(4,128)}, f32[4,4096]{1,0:T(4,128)S(1)}, u32[]{:S(2)}, u32[]{:S(2)}) collective-permute-start(f32[4,4096]{1,0:T(4,128)} %param.10), channel_id=1, source_target_pairs={{0,6},{1,7},{2,4},{3,5},{4,2},{5,3},{6,0},{7,1},{8,14},{9,15},{10,... | collective-permute-start | bytes 196616 | tf_op jit(solution)/shard_map/ppermute | solution.py:278
  6.2 13.9 %collective-permute-start.1 = (f32[4,4096]{1,0:T(4,128)}, f32[4,4096]{1,0:T(4,128)S(1)}, u32[]{:S(2)}, u32[]{:S(2)}) collective-permute-start(f32[4,4096]{1,0:T(4,128)} %param.10), channel_id=1, source_target_pairs={{0,4},{1,5},{2,6},{3,7},{4,0},{5,1},{6,2},{7,3},{8,12},{9,13},{10,... | collective-permute-start | bytes 196616 | tf_op jit(solution)/shard_map/ppermute | solution.py:278
  6.3 4.8 %collective-permute-start.6 = (f32[8,2048]{1,0:T(8,128)}, f32[8,2048]{1,0:T(8,128)S(1)}, u32[]{:S(2)}, u32[]{:S(2)}) collective-permute-start(f32[8,2048]{1,0:T(8,128)} %param.11), channel_id=1, source_target_pairs={{0,8},{8,0},{16,24},{24,16},{1,9},{9,1},{17,25},{25,17},{2,10},{10... | collective-permute-start | bytes 196616 | tf_op jit(solution)/shard_map/ppermute | solution.py:278
  7.8 7.8 %collective-permute-start.8 = (f32[8,2048]{1,0:T(8,128)}, f32[8,2048]{1,0:T(8,128)S(1)}, u32[]{:S(2)}, u32[]{:S(2)}) collective-permute-start(f32[8,2048]{1,0:T(8,128)} %param.11), channel_id=1, source_target_pairs={{0,24},{8,16},{16,8},{24,0},{1,25},{9,17},{17,9},{25,1},{2,26},{10... | collective-permute-start | bytes 196616 | tf_op jit(solution)/shard_map/ppermute | solution.py:278
  9.4 19.7 %copy-start.8 = (s32[4,2]{0,1:T(2,128)S(1)}, s32[4,2]{0,1:T(2,128)}, u32[]{:S(2)}) copy-start(s32[4,2]{0,1:T(2,128)} %param.16) | copy-start | bytes 100
  11.1 4.5 %collective-permute-start.7 = (f32[8,2048]{1,0:T(8,128)}, f32[8,2048]{1,0:T(8,128)S(1)}, u32[]{:S(2)}, u32[]{:S(2)}) collective-permute-start(f32[8,2048]{1,0:T(8,128)} %param.11), channel_id=1, source_target_pairs={{0,16},{8,24},{16,0},{24,8},{1,17},{9,25},{17,1},{25,9},{2,18},{10... | collective-permute-start | bytes 196616 | tf_op jit(solution)/shard_map/ppermute | solution.py:278
  15.7 14.8 %copy-start.2 = (f32[4,8,2048]{2,1,0:T(8,128)}, f32[4,8,2048]{2,1,0:T(8,128)S(1)}, u32[]{:S(2)}) copy-start(f32[4,8,2048]{2,1,0:T(8,128)S(1)} %bitcast_dynamic-update-slice_fusion.2) | copy-start | bytes 786436
  15.7 14.0 %collective-permute-start.10 = (f32[32,128]{1,0:T(8,128)S(1)}, f32[32,128]{1,0:T(8,128)S(1)}, u32[]{:S(2)}, u32[]{:S(2)}) collective-permute-start(f32[32,128]{1,0:T(8,128)S(1)} %get-tuple-element.28), channel_id=1, source_target_pairs={{1,0},{2,1},{3,2},{4,3},{5,4},{6,5},{7,6},{9,8},{10,9},{11,10},{12... | collective-permute-start | bytes 49160 | tf_op jit(solution)/shard_map/ppermute | solution.py:286
  17.0 12.7 %collective-permute-start.9 = (f32[32,128]{1,0:T(8,128)S(1)}, f32[32,128]{1,0:T(8,128)S(1)}, u32[]{:S(2)}, u32[]{:S(2)}) collective-permute-start(f32[32,128]{1,0:T(8,128)S(1)} %get-tuple-element.29), channel_id=1, source_target_pairs={{0,1},{1,2},{2,3},{3,4},{4,5},{5,6},{6,7},{8,9},{9,10},{10,11},{11... | collective-permute-start | bytes 49160 | tf_op jit(solution)/shard_map/ppermute | solution.py:285
  20.2 2.8 %collective-permute-start.3 = (f32[4,4,4096]{2,1,0:T(4,128)S(1)}, f32[4,4,4096]{2,1,0:T(4,128)S(1)}, u32[]{:S(2)}, u32[]{:S(2)}) collective-permute-start(f32[4,4,4096]{2,1,0:T(4,128)S(1)} %bitcast_dynamic-update-slice_fusion.6), channel_id=1, source_target_pairs={{0,1},{1,0},{2,3},{3,2},{4,5},{5,4},{6,7},{7,6},{8,9},{9,8},{10,11... | collective-permute-start | bytes 786440 | tf_op jit(solution)/shard_map/ppermute | solution.py:278
  23.2 7.3 %copy-start = (f32[32,4096]{1,0:T(8,128)}, f32[32,4096]{1,0:T(8,128)S(1)}, u32[]{:S(2)}) copy-start(f32[32,4096]{1,0:T(8,128)S(1)} %reshape.44.left) | copy-start | bytes 1572868
  23.2 6.5 %collective-permute-start.5 = (f32[32,128]{1,0:T(8,128)S(1)}, f32[32,128]{1,0:T(8,128)S(1)}, u32[]{:S(2)}, u32[]{:S(2)}) collective-permute-start(f32[32,128]{1,0:T(8,128)S(1)} %get-tuple-element.26), channel_id=1, source_target_pairs={{8,0},{16,8},{24,16},{9,1},{17,9},{25,17},{10,2},{18,10},{26,18},{... | collective-permute-start | bytes 49160 | tf_op jit(solution)/shard_map/ppermute | solution.py:286
  24.5 6.0 %collective-permute-start.4 = (f32[32,128]{1,0:T(8,128)S(1)}, f32[32,128]{1,0:T(8,128)S(1)}, u32[]{:S(2)}, u32[]{:S(2)}) collective-permute-start(f32[32,128]{1,0:T(8,128)S(1)} %get-tuple-element.27), channel_id=1, source_target_pairs={{0,8},{8,16},{16,24},{1,9},{9,17},{17,25},{2,10},{10,18},{18,26},{... | collective-permute-start | bytes 49160 | tf_op jit(solution)/shard_map/ppermute | solution.py:285
  29.7 0.8 copy-start.4
  29.7 0.8 copy-start.5
  29.7 0.8 copy-start.6
  30.5 0.6 copy-start.7
  57.5 10.6 %copy-start.1 = (f32[2,2,4,4,8192]{4,3,2,1,0:T(4,128)S(1)}, f32[2,2,4,4,8192]{4,3,2,1,0:T(4,128)}, u32[]{:S(2)}) copy-start(f32[2,2,4,4,8192]{4,3,2,1,0:T(4,128)} %get-tuple-element.6) | copy-start | bytes 6291460
  59.0 16.4 %copy-start.3 = (f32[2,4,8,4096]{3,2,1,0:T(8,128)S(1)}, f32[2,4,8,4096]{3,2,1,0:T(8,128)}, u32[]{:S(2)}) copy-start(f32[2,4,8,4096]{3,2,1,0:T(8,128)} %get-tuple-element.9) | copy-start | bytes 3145732
  59.0 9.2 %collective-permute-start.11 = (f32[2,4,4,8192]{3,2,1,0:T(4,128)S(1)}, f32[2,4,4,8192]{3,2,1,0:T(4,128)S(1)}, u32[]{:S(2)}, u32[]{:S(2)}) collective-permute-start(f32[2,4,4,8192]{3,2,1,0:T(4,128)S(1)} %slice_bitcast_fusion.1), channel_id=1, source_target_pairs={{0,1},{1,0},{2,3},{3,2},{4,5},{5,4},{6,7},{7,6},{8,9},{9,8},{10,11... | collective-permute-start | bytes 3145736 | tf_op jit(solution)/shard_map/ppermute | solution.py:278
  68.5 16.3 %collective-permute-start.14 = (f32[2,4,8192]{2,1,0:T(4,128)S(1)}, f32[2,4,8192]{2,1,0:T(4,128)S(1)}, u32[]{:S(2)}, u32[]{:S(2)}) collective-permute-start(f32[2,4,8192]{2,1,0:T(4,128)S(1)} %pad_maximum_fusion.1), channel_id=1, source_target_pairs={{0,4},{1,5},{2,6},{3,7},{4,0},{5,1},{6,2},{7,3},{8,12},{9,13},{10,... | collective-permute-start | bytes 786440 | tf_op jit(solution)/shard_map/ppermute | solution.py:278
  75.3 13.7 %collective-permute-start.12 = (f32[2,4,8192]{2,1,0:T(4,128)S(1)}, f32[2,4,8192]{2,1,0:T(4,128)S(1)}, u32[]{:S(2)}, u32[]{:S(2)}) collective-permute-start(f32[2,4,8192]{2,1,0:T(4,128)S(1)} %pad_maximum_fusion), channel_id=1, source_target_pairs={{0,2},{1,3},{2,0},{3,1},{4,6},{5,7},{6,4},{7,5},{8,10},{9,11},{10,... | collective-permute-start | bytes 786440 | tf_op jit(solution)/shard_map/ppermute | solution.py:278
  75.5 14.5 %collective-permute-start.18 = (f32[2,8,4096]{2,1,0:T(8,128)S(1)}, f32[2,8,4096]{2,1,0:T(8,128)S(1)}, u32[]{:S(2)}, u32[]{:S(2)}) collective-permute-start(f32[2,8,4096]{2,1,0:T(8,128)S(1)} %pad_maximum_fusion.4), channel_id=1, source_target_pairs={{0,16},{8,24},{16,0},{24,8},{1,17},{9,25},{17,1},{25,9},{2,18},{10... | collective-permute-start | bytes 786440 | tf_op jit(solution)/shard_map/ppermute | solution.py:278
  84.0 7.6 %collective-permute-start.16 = (f32[2,8,4096]{2,1,0:T(8,128)S(1)}, f32[2,8,4096]{2,1,0:T(8,128)S(1)}, u32[]{:S(2)}, u32[]{:S(2)}) collective-permute-start(f32[2,8,4096]{2,1,0:T(8,128)S(1)} %pad_maximum_fusion.3), channel_id=1, source_target_pairs={{0,8},{8,0},{16,24},{24,16},{1,9},{9,1},{17,25},{25,17},{2,10},{10... | collective-permute-start | bytes 786440 | tf_op jit(solution)/shard_map/ppermute | solution.py:278
  89.0 9.0 %collective-permute-start.13 = (f32[1,4,8192]{2,1,0:T(4,128)S(1)}, f32[1,4,8192]{2,1,0:T(4,128)S(1)}, u32[]{:S(2)}, u32[]{:S(2)}) collective-permute-start(f32[1,4,8192]{2,1,0:T(4,128)S(1)} %get-tuple-element.20), channel_id=1, source_target_pairs={{0,4},{1,5},{2,6},{3,7},{4,0},{5,1},{6,2},{7,3},{8,12},{9,13},{10,... | collective-permute-start | bytes 393224 | tf_op jit(solution)/shard_map/ppermute | solution.py:278
  89.1 8.9 %collective-permute-start.15 = (f32[1,4,8192]{2,1,0:T(4,128)S(1)}, f32[1,4,8192]{2,1,0:T(4,128)S(1)}, u32[]{:S(2)}, u32[]{:S(2)}) collective-permute-start(f32[1,4,8192]{2,1,0:T(4,128)S(1)} %get-tuple-element.21), channel_id=1, source_target_pairs={{0,2},{1,3},{2,0},{3,1},{4,6},{5,7},{6,4},{7,5},{8,10},{9,11},{10,... | collective-permute-start | bytes 393224 | tf_op jit(solution)/shard_map/ppermute | solution.py:278
  91.6 9.4 %collective-permute-start.17 = (f32[1,8,4096]{2,1,0:T(8,128)S(1)}, f32[1,8,4096]{2,1,0:T(8,128)S(1)}, u32[]{:S(2)}, u32[]{:S(2)}) collective-permute-start(f32[1,8,4096]{2,1,0:T(8,128)S(1)} %get-tuple-element.12), channel_id=1, source_target_pairs={{0,16},{8,24},{16,0},{24,8},{1,17},{9,25},{17,1},{25,9},{2,18},{10... | collective-permute-start | bytes 393224 | tf_op jit(solution)/shard_map/ppermute | solution.py:278
  98.0 5.0 %collective-permute-start.19 = (f32[1,8,4096]{2,1,0:T(8,128)S(1)}, f32[1,8,4096]{2,1,0:T(8,128)S(1)}, u32[]{:S(2)}, u32[]{:S(2)}) collective-permute-start(f32[1,8,4096]{2,1,0:T(8,128)S(1)} %get-tuple-element.13), channel_id=1, source_target_pairs={{0,8},{8,0},{16,24},{24,16},{1,9},{9,1},{17,25},{25,17},{2,10},{10... | collective-permute-start | bytes 393224 | tf_op jit(solution)/shard_map/ppermute | solution.py:278
where the time goes:
time: 104 us
  starting transfers between devices  50.9 us (49%)
  Pallas kernels  26.4 us (25%)
  waiting for transfers between devices  18.3 us (18%)
  local copies, waits for them, and re-layouts  4.96 us (5%)
  other arithmetic  2.14 us (2%)
    ppermute x16, starting transfers between devices, swap(): lax.ppermute(x, axis, [(i, i ^ distance) for i in range(lax.axis_size(axi...  40.8 us
    pallas_call x1, Pallas kernels, on_device(): pl.pallas_call(functools.partial(step, eta=4.0 * TILE / (SPT * TILES)), o...  26.4 us
    ppermute x16, waiting for transfers between devices, swap(): lax.ppermute(x, axis, [(i, i ^ distance) for i in range(lax.axis_size(axi...  17.6 us
    ppermute x2, starting transfers between devices, from_neighbours(): low = lax.ppermute(x[:, x.shape[1] - EDGE:], axis, forward)  7.58 us
    ppermute x2, starting transfers between devices, from_neighbours(): high = lax.ppermute(x[:, :EDGE], axis, backward)  2.58 us
  transfers between devices with their start and end apart: 20, of which 10 were waited for; matrix products, arithmetic and copies ran while one was open for 4% of the time, Pallas kernels for 0%

commit v1 on v0

--- a/solution.py
+++ b/solution.py
@@ -144,9 +144,7 @@
 
 def step(
     mask,
-    left_low,
     left,
-    left_high,
     right_low,
     right,
     right_high,
@@ -157,9 +155,9 @@
     rows,
     cols,
     values,
-    left_parts,
+    left_kept,
+    left_sent,
     right_parts,
-    left_padded,
     right_padded,
     left_table,
     right_table,
@@ -174,18 +172,17 @@
     rank = left.shape[0]
     tile_rows, tile_cols, samples = rows.shape
     me_row, me_col = lax.axis_index("row"), lax.axis_index("col")
-    left_rank, right_rank = left_parts.shape[3], right_parts.shape[2]
-    pad(left_low, left, left_high, left_padded)
+    left_rank, right_rank = left_kept.shape[2], right_parts.shape[1]
     pad(right_low, right, right_high, right_padded)
     for a in range(tile_rows):
         interpolate(
-            left_padded,
+            left,
             stencil_left,
             weights_left,
             keep_split(left_table, a),
             left_out,
             me_col,
-            me_row * left.shape[1],
+            me_row * (left.shape[1] - 2 * EDGE),
             a,
             left_rank,
         )
@@ -249,29 +246,27 @@
         adds(live[count - 1], batches - 1)
 
     def left_group(i, _):
-        half = left_parts.shape[4]
+        half = left_kept.shape[3]
         for h in range(2):
             at = pl.multiple_of(i * 512, 512)
             part = left_out[:, pl.ds(h * half + at, 512)]
-            for c in range(rank // left_rank):
-                left_parts[h, (c % 2) ^ (me_col % 2), (c // 2) ^ (me_col // 2), :, pl.ds(at, 512)] = (
-                    part[c * left_rank : (c + 1) * left_rank]
-                )
+            for g in range(rank // left_rank // 2):
+                low = part[2 * g * left_rank : (2 * g + 1) * left_rank]
+                high = part[(2 * g + 1) * left_rank : (2 * g + 2) * left_rank]
+                to = (h, g ^ (me_col // 2), slice(None), pl.ds(at, 512))
+                left_kept[to] = jnp.where(me_col % 2 == 0, low, high)
+                left_sent[to] = jnp.where(me_col % 2 == 0, high, low)
         return 0
 
     def right_group(i, _):
-        half = right_parts.shape[3]
-        for h in range(2):
-            at = pl.multiple_of(i * 512, 512)
-            part = right_out[:, pl.ds(h * half + at, 512)]
-            for r in range(rank // right_rank):
-                right_parts[h, r ^ me_row, :, pl.ds(at, 512)] = part[
-                    r * right_rank : (r + 1) * right_rank
-                ]
+        at = pl.ds(pl.multiple_of(i * 512, 512), 512)
+        part = right_out[:, at]
+        for r in range(rank // right_rank):
+            right_parts[r ^ me_row, :, at] = part[r * right_rank : (r + 1) * right_rank]
         return 0
 
-    lax.fori_loop(0, left_parts.shape[4] // 512, left_group, 0)
-    lax.fori_loop(0, right_parts.shape[3] // 512, right_group, 0)
+    lax.fori_loop(0, left_kept.shape[3] // 512, left_group, 0)
+    lax.fori_loop(0, right_parts.shape[2] // 512, right_group, 0)
 
 
 def swap(x, axis, distance):
@@ -298,14 +293,11 @@
     return out
 
 
-def halve(parts, axis, distances):
-    parts = {j: parts[j] for j in range(parts.shape[0])}
-    for step in distances:
-        kept = [j for j in parts if not j & step]
-        sent = jnp.stack([parts[j ^ step] for j in kept])
-        came = swap(sent, axis[0], step * axis[1])
-        parts = {j: parts[j] + came[i] for i, j in enumerate(kept)}
-    return parts[0]
+def halve(parts, axis, step):
+    kept = [j for j in parts if not j & step]
+    sent = jnp.stack([parts[j ^ step] for j in kept])
+    came = swap(sent, axis[0], step * axis[1])
+    return {j: parts[j] + came[i] for i, j in enumerate(kept)}
 
 
 def on_device(
@@ -325,26 +317,32 @@
     left_rank, left_width = coarse_left.shape
     right_rank, right_width = coarse_right.shape
     rank = left_rank * cols
-    half = gather(coarse_left, "col", col // 2, cols // 2, 2)
-    right = gather(coarse_right, "row", row, rows, 1).reshape(rank, right_width)
+    edges = jnp.concatenate([coarse_left[:, :EDGE], coarse_left[:, left_width - EDGE :]], axis=1)
+    packed = jnp.concatenate([coarse_right, edges.reshape(right_rank, -1)], axis=1)
+    packed = gather(packed, "row", row, rows, 1)
+    edges = packed[:, :, right_width:].reshape(rows, left_rank, 2, EDGE)
+    low = jnp.where(row > 0, edges[jnp.maximum(row - 1, 0), :, 1], 0.0)
+    high = jnp.where(row < rows - 1, edges[jnp.minimum(row + 1, rows - 1), :, 0], 0.0)
+    own = jnp.concatenate([low, coarse_left, high], axis=1)
+    half = gather(own, "col", col // 2, cols // 2, 2)
+    right = packed[:, :, :right_width].reshape(rank, right_width)
     right_low, right_high = from_neighbours(right, "col")
     other = swap(half, "col", 1)
-    left = jnp.zeros((cols // 2, 2, left_rank, left_width), jnp.float32)
-    left = put(put(left, half, col % 2, 1), other, 1 - col % 2, 1).reshape(rank, left_width)
-    left_low, left_high = from_neighbours(left, "row")
+    left = jnp.zeros((cols // 2, 2) + own.shape, jnp.float32)
+    left = put(put(left, half, col % 2, 1), other, 1 - col % 2, 1).reshape(rank, -1)
     tile_rows, tile_cols, _ = sample_rows.shape
     smem = pl.BlockSpec(memory_space=pltpu.SMEM)
     vmem = pl.BlockSpec(memory_space=pltpu.VMEM)
-    left_parts, right_parts = pl.pallas_call(
+    left_kept, left_sent, right_parts = pl.pallas_call(
         functools.partial(step, eta=4.0 * TILE / (SPT * TILES)),
         out_shape=(
-            jax.ShapeDtypeStruct((2, 2, cols // 2, left_rank, tile_rows * TILE // 2), jnp.float32),
-            jax.ShapeDtypeStruct((2, rows, right_rank, tile_cols * TILE // 2), jnp.float32),
+            jax.ShapeDtypeStruct((2, cols // 2, left_rank, tile_rows * TILE // 2), jnp.float32),
+            jax.ShapeDtypeStruct((2, cols // 2, left_rank, tile_rows * TILE // 2), jnp.float32),
+            jax.ShapeDtypeStruct((rows, right_rank, tile_cols * TILE), jnp.float32),
         ),
-        in_specs=[smem] + [vmem] * 13,
-        out_specs=(vmem, vmem),
+        in_specs=[smem] + [vmem] * 11,
+        out_specs=(vmem, vmem, vmem),
         scratch_shapes=[
-            pltpu.VMEM((rank, left_width + 2 * EDGE), jnp.float32),
             pltpu.VMEM((rank, right_width + 2 * EDGE), jnp.float32),
             pltpu.VMEM((tile_rows, TILE // CHUNK * rank, 2 * CHUNK), jnp.bfloat16),
             pltpu.VMEM((tile_cols, rank, TILE), jnp.float32),
@@ -357,9 +355,7 @@
         compiler_params=pltpu.CompilerParams(vmem_limit_bytes=60 * 1024 * 1024),
     )(
         tile_mask,
-        left_low,
         left,
-        left_high,
         right_low,
         right,
         right_high,
@@ -371,14 +367,23 @@
         sample_cols,
         sample_values,
     )
-    came = swap(left_parts[:, 1], "col", 1)
-    left_added, right_parts = lax.optimization_barrier((left_parts[:, 0] + came, right_parts))
-    left_sums, right_sums = [], []
-    for h in range(2):
-        turned = slice(None, None, 1 - 2 * h)
-        left_sums.append(halve(left_added[h], ("col", 2), bits(cols // 2)[turned]))
-        right_sums.append(halve(right_parts[h], ("row", 1), bits(rows)[turned]))
-    return (jnp.concatenate(left_sums, axis=1), jnp.concatenate(right_sums, axis=1))
+    left_added, right_parts = lax.optimization_barrier(
+        (left_kept + swap(left_sent, "col", 1), right_parts)
+    )
+    sums = [
+        [left_added[0], ("col", 2), bits(cols // 2)],
+        [left_added[1], ("col", 2), bits(cols // 2)[::-1]],
+        [right_parts, ("row", 1), bits(rows)],
+    ]
+    held = [{j: parts[j] for j in range(parts.shape[0])} for parts, _, _ in sums]
+    for turn in range(max(len(steps) for _, _, steps in sums)):
+        if turn:
+            held = lax.optimization_barrier(held)
+        for i, (_, axis, steps) in enumerate(sums):
+            if turn < len(steps):
+                held[i] = halve(held[i], axis, steps[turn])
+    left_low, left_high, right = (parts[0] for parts in held)
+    return (jnp.concatenate([left_low, left_high], axis=1), right)
 
 
 def bits(count):

time: 104 us -> 97.6 us (0.938)
  starting transfers between devices: 50.9 us -> 35.2 us
  waiting for transfers between devices: 18.3 us -> 25.4 us
  other arithmetic: 2.14 us -> 3.49 us
    ppermute x16 -> x14, starting transfers between devices: 40.8 us -> 30.9 us  [swap(): lax.ppermute(x, axis, [(i, i ^ distance) for i in range(lax.axis_size(axi...]
    ppermute x16 -> x14, waiting for transfers between devices: 17.6 us -> 25.4 us  [swap(): lax.ppermute(x, axis, [(i, i ^ distance) for i in range(lax.axis_size(axi...]
    ppermute x2 -> x1, starting transfers between devices: 7.58 us -> 3.03 us  [from_neighbours(): low = lax.ppermute(x[:, x.shape[1] - EDGE:], axis, forward)]
    unnamed x19 -> x14, local copies, waits for them, and re-layouts: 1.26 us -> 3.56 us
    add x5 -> x6, other arithmetic: 0.51 us -> 2.5 us  [the longest x1 1.5 us: on_device(): left_kept + swap(left_sent, 'col', 1)]
    dynamic_update_slice x10 -> x9, local copies, waits for them, and re-layouts: 1.87 us -> 0.18 us  [put(): return lax.dynamic_update_index_in_dim(buffer, x, index, axis)]
    squeeze x1 -> x0, local copies, waits for them, and re-layouts: 1.44 us -> none  [on_device(): came = swap(left_parts[:, 1], 'col', 1)]
    ppermute x2 -> x1, starting transfers between devices: 2.58 us -> 1.28 us  [from_neighbours(): high = lax.ppermute(x[:, :EDGE], axis, backward)]
  transfers between devices with their start and end apart: 20 -> 16, of which waited for: 10 -> 8; matrix products, arithmetic and copies ran while one was open for 4% -> 3% of each run, Pallas kernels for 0% -> 0%
where the time goes in v1:
time: 97.6 us; the launch traced here: 97.2 us
  starting transfers between devices  35.2 us (36%)
  Pallas kernels  26.4 us (27%)
  waiting for transfers between devices  25.4 us (26%)
  local copies, waits for them, and re-layouts  5.69 us (6%)
  other arithmetic  3.49 us (4%)
  between operations  0.98 us (1%)
    ppermute x14, starting transfers between devices, swap(): lax.ppermute(x, axis, [(i, i ^ distance) for i in range(lax.axis_size(axi...  30.9 us
    pallas_call x1, Pallas kernels, on_device(): pl.pallas_call(functools.partial(step, eta=4.0 * TILE / (SPT * TILES)), o...  26.4 us
    ppermute x14, waiting for transfers between devices, swap(): lax.ppermute(x, axis, [(i, i ^ distance) for i in range(lax.axis_size(axi...  25.4 us
    unnamed x14, local copies, waits for them, and re-layouts  3.56 us
    ppermute x1, starting transfers between devices, from_neighbours(): low = lax.ppermute(x[:, x.shape[1] - EDGE:], axis, forward)  3.03 us
  transfers between devices with their start and end apart: 16, of which 8 were waited for; matrix products, arithmetic and copies ran while one was open for 3% of the time, Pallas kernels for 0%

profile of v1, /device:TPU:0, one launch (start us, length us, event | category | flops | bytes accessed | tf_op | source)
XLA Modules:
  0.0 97.2 jit_solution(3891681996499176488)
XLA Ops:
  0.6 0.7 fusion.8
  1.4 0.8 constant_dynamic-update-slice_fusion.1
  2.2 3.9 %collective-permute-start.2 = (f32[8,2176]{1,0:T(8,128)S(1)}, f32[8,2176]{1,0:T(8,128)S(1)}, u32[]{:S(2)}, u32[]{:S(2)}) collective-permute-start(f32[8,2176]{1,0:T(8,128)S(1)} %constant_dynamic-update-slice_fusion), channel_id=1, source_target_pairs={{0,24},{8,16},{16,8},{24,0},{1,25},{9,17},{17,9},{25,1},{2,26},{10... | collective-permute-start | bytes 208904 | tf_op jit(solution)/shard_map/ppermute | solution.py:273
  6.1 0.5 collective-permute-start.1
  6.9 0.7 copy-done.5
  7.5 0.7 copy.15.mask
  8.2 2.7 %collective-permute-done = f32[8,2176]{1,0:T(8,128)S(1)} collective-permute-done((f32[8,2176]{1,0:T(8,128)S(1)}, f32[8,2176]{1,0:T(8,128)S(1)}, u32[]{:S(2)}, u32[]{:S(2)}) %collective-permute-start) | collective-permute-done | bytes 69664 | tf_op jit(solution)/shard_map/ppermute | solution.py:273
  11.1 0.8 copy-done.2
  11.9 2.7 %collective-permute-start.4 = (f32[4,4352]{1,0:T(4,128)S(1)}, f32[4,4352]{1,0:T(4,128)S(1)}, u32[]{:S(2)}, u32[]{:S(2)}) collective-permute-start(f32[4,4352]{1,0:T(4,128)S(1)} %pad_maximum_fusion.4), channel_id=1, source_target_pairs={{0,4},{1,5},{2,6},{3,7},{4,0},{5,1},{6,2},{7,3},{8,12},{9,13},{10,... | collective-permute-start | bytes 208904 | tf_op jit(solution)/shard_map/ppermute | solution.py:273
  14.5 1.6 %collective-permute-start.3 = (f32[4,4352]{1,0:T(4,128)S(1)}, f32[4,4352]{1,0:T(4,128)S(1)}, u32[]{:S(2)}, u32[]{:S(2)}) collective-permute-start(f32[4,4352]{1,0:T(4,128)S(1)} %pad_maximum_fusion.4), channel_id=1, source_target_pairs={{0,2},{1,3},{2,0},{3,1},{4,6},{5,7},{6,4},{7,5},{8,10},{9,11},{10,... | collective-permute-start | bytes 208904 | tf_op jit(solution)/shard_map/ppermute | solution.py:273
  16.3 1.3 %collective-permute-start.8 = (f32[32,128]{1,0:T(8,128)S(1)}, f32[32,128]{1,0:T(8,128)S(1)}, u32[]{:S(2)}, u32[]{:S(2)}) collective-permute-start(f32[32,128]{1,0:T(8,128)S(1)} %get-tuple-element.38), channel_id=1, source_target_pairs={{1,0},{2,1},{3,2},{4,3},{5,4},{6,5},{7,6},{9,8},{10,9},{11,10},{12... | collective-permute-start | bytes 49160 | tf_op jit(solution)/shard_map/ppermute | solution.py:281
  17.6 3.0 %collective-permute-start.7 = (f32[32,128]{1,0:T(8,128)S(1)}, f32[32,128]{1,0:T(8,128)S(1)}, u32[]{:S(2)}, u32[]{:S(2)}) collective-permute-start(f32[32,128]{1,0:T(8,128)S(1)} %get-tuple-element.39), channel_id=1, source_target_pairs={{0,1},{1,2},{2,3},{3,4},{4,5},{5,6},{6,7},{8,9},{9,10},{10,11},{11... | collective-permute-start | bytes 49160 | tf_op jit(solution)/shard_map/ppermute | solution.py:280
  20.8 1.5 %collective-permute-done.5 = f32[4,4352]{1,0:T(4,128)S(1)} collective-permute-done((f32[4,4352]{1,0:T(4,128)S(1)}, f32[4,4352]{1,0:T(4,128)S(1)}, u32[]{:S(2)}, u32[]{:S(2)}) %collective-permute-start.5) | collective-permute-done | bytes 69664 | tf_op jit(solution)/shard_map/ppermute | solution.py:273
  22.6 1.4 %collective-permute-done.6 = f32[4,4,4352]{2,1,0:T(4,128)S(1)} collective-permute-done((f32[4,4,4352]{2,1,0:T(4,128)S(1)}, f32[4,4,4352]{2,1,0:T(4,128)S(1)}, u32[]{:S(2)}, u32[]{:S(2)}) %collective-permute-start.6) | collective-permute-done | bytes 278560 | tf_op jit(solution)/shard_map/ppermute | solution.py:273
  24.0 1.0 %reshape.44.left = f32[32,4352]{1,0:T(8,128)} reshape(f32[4,2,4,4352]{3,2,1,0:T(4,128)S(1)} %bitcast_dynamic-update-slice_fusion.1) | data formatting | bytes 1114112 | tf_op jit(solution)/shard_map/reshape | solution.py:332
  25.0 0.6 copy-done.3
  25.6 26.4 %shard_map.113 = (f32[2,4,4,8192]{3,2,1,0:T(4,128)}, f32[2,4,4,8192]{3,2,1,0:T(4,128)}, f32[4,8,8192]{2,1,0:T(8,128)}) custom-call(s32[4,2]{1,0:T(4,128)} %copy.15.mask, f32[32,4352]{1,0:T(8,128)} %reshape.44.left, f32[32,128]{1,0:T(8,128)} %copy-done.4, f32[32,2048]{1,0:T(8,128)} %copy-done, f32[32,128]{1,0:T(8,128)} %copy-done.3, s32[16,8,128]{2,1,0:T(8,128)} %bitcast.77, ...), custom_call_target="tpu_custom_call" | custom-call | tf_op jit(solution)/shard_map/pallas_call | solution.py:336
  52.1 7.7 %collective-permute-start.9 = (f32[2,4,4,8192]{3,2,1,0:T(4,128)}, f32[2,4,4,8192]{3,2,1,0:T(4,128)S(1)}, u32[]{:S(2)}, u32[]{:S(2)}) collective-permute-start(f32[2,4,4,8192]{3,2,1,0:T(4,128)} %get-tuple-element.14), channel_id=1, source_target_pairs={{0,1},{1,0},{2,3},{3,2},{4,5},{5,4},{6,7},{7,6},{8,9},{9,8},{10,11... | collective-permute-start | bytes 3145736 | tf_op jit(solution)/shard_map/ppermute | solution.py:273
  59.8 2.5 %collective-permute-done.9 = f32[2,4,4,8192]{3,2,1,0:T(4,128)S(1)} collective-permute-done((f32[2,4,4,8192]{3,2,1,0:T(4,128)}, f32[2,4,4,8192]{3,2,1,0:T(4,128)S(1)}, u32[]{:S(2)}, u32[]{:S(2)}) %collective-permute-start.9) | collective-permute-done | bytes 1048608 | tf_op jit(solution)/shard_map/ppermute | solution.py:273
  62.3 1.5 %add.97 = f32[2,4,4,8192]{3,2,1,0:T(4,128)S(1)} add(f32[2,4,4,8192]{3,2,1,0:T(4,128)} %get-tuple-element.13, f32[2,4,4,8192]{3,2,1,0:T(4,128)S(1)} %collective-permute-done.9) | non-fusion elementwise | flops 262144 | bytes 3145728 | tf_op jit(solution)/shard_map/add | solution.py:371
  63.9 0.3 collective-permute-start.10
  64.3 5.8 %collective-permute-start.11 = (f32[2,4,8192]{2,1,0:T(4,128)S(1)}, f32[2,4,8192]{2,1,0:T(4,128)S(1)}, u32[]{:S(2)}, u32[]{:S(2)}) collective-permute-start(f32[2,4,8192]{2,1,0:T(4,128)S(1)} %pad_maximum_fusion.2), channel_id=1, source_target_pairs={{0,4},{1,5},{2,6},{3,7},{4,0},{5,1},{6,2},{7,3},{8,12},{9,13},{10,... | collective-permute-start | bytes 786440 | tf_op jit(solution)/shard_map/ppermute | solution.py:273
  70.2 0.7 collective-permute-start.12
  70.8 7.4 %collective-permute-done.10 = f32[2,4,8192]{2,1,0:T(4,128)S(1)} collective-permute-done((f32[2,4,8192]{2,1,0:T(4,128)S(1)}, f32[2,4,8192]{2,1,0:T(4,128)S(1)}, u32[]{:S(2)}, u32[]{:S(2)}) %collective-permute-start.10) | collective-permute-done | bytes 262176 | tf_op jit(solution)/shard_map/ppermute | solution.py:273
  78.3 5.6 %collective-permute-done.12 = f32[2,8,8192]{2,1,0:T(8,128)S(1)} collective-permute-done((f32[2,8,8192]{2,1,0:T(8,128)S(1)}, f32[2,8,8192]{2,1,0:T(8,128)S(1)}, u32[]{:S(2)}, u32[]{:S(2)}) %collective-permute-start.12) | collective-permute-done | bytes 524320 | tf_op jit(solution)/shard_map/ppermute | solution.py:273
  84.0 1.2 %collective-permute-start.13 = (f32[1,4,8192]{2,1,0:T(4,128)S(1)}, f32[1,4,8192]{2,1,0:T(4,128)S(1)}, u32[]{:S(2)}, u32[]{:S(2)}) collective-permute-start(f32[1,4,8192]{2,1,0:T(4,128)S(1)} %bitcast.76), channel_id=1, source_target_pairs={{0,4},{1,5},{2,6},{3,7},{4,0},{5,1},{6,2},{7,3},{8,12},{9,13},{10,... | collective-permute-start | bytes 393224 | tf_op jit(solution)/shard_map/ppermute | solution.py:273
  85.2 1.5 %collective-permute-start.14 = (f32[1,4,8192]{2,1,0:T(4,128)S(1)}, f32[1,4,8192]{2,1,0:T(4,128)S(1)}, u32[]{:S(2)}, u32[]{:S(2)}) collective-permute-start(f32[1,4,8192]{2,1,0:T(4,128)S(1)} %bitcast.75), channel_id=1, source_target_pairs={{0,2},{1,3},{2,0},{3,1},{4,6},{5,7},{6,4},{7,5},{8,10},{9,11},{10,... | collective-permute-start | bytes 393224 | tf_op jit(solution)/shard_map/ppermute | solution.py:273
  86.7 4.6 %collective-permute-start.15 = (f32[1,8,8192]{2,1,0:T(8,128)S(1)}, f32[1,8,8192]{2,1,0:T(8,128)S(1)}, u32[]{:S(2)}, u32[]{:S(2)}) collective-permute-start(f32[1,8,8192]{2,1,0:T(8,128)S(1)} %bitcast.74), channel_id=1, source_target_pairs={{0,16},{8,24},{16,0},{24,8},{1,17},{9,25},{17,1},{25,9},{2,18},{10... | collective-permute-start | bytes 786440 | tf_op jit(solution)/shard_map/ppermute | solution.py:273
  91.3 0.8 collective-permute-done.13
  92.2 0.8 pad_maximum_fusion.3
  93.0 3.5 %collective-permute-done.15 = f32[1,8,8192]{2,1,0:T(8,128)S(1)} collective-permute-done((f32[1,8,8192]{2,1,0:T(8,128)S(1)}, f32[1,8,8192]{2,1,0:T(8,128)S(1)}, u32[]{:S(2)}, u32[]{:S(2)}) %collective-permute-start.15) | collective-permute-done | bytes 262176 | tf_op jit(solution)/shard_map/ppermute | solution.py:273
  96.5 0.7 bitcast_add_fusion
  (50 shorter events, 1.4 us)
Async XLA Ops:
  2.2 8.8 %collective-permute-start.2 = (f32[8,2176]{1,0:T(8,128)S(1)}, f32[8,2176]{1,0:T(8,128)S(1)}, u32[]{:S(2)}, u32[]{:S(2)}) collective-permute-start(f32[8,2176]{1,0:T(8,128)S(1)} %constant_dynamic-update-slice_fusion), channel_id=1, source_target_pairs={{0,24},{8,16},{16,8},{24,0},{1,25},{9,17},{17,9},{25,1},{2,26},{10... | collective-permute-start | bytes 208904 | tf_op jit(solution)/shard_map/ppermute | solution.py:273
  6.1 4.8 %collective-permute-start.1 = (f32[8,2176]{1,0:T(8,128)S(1)}, f32[8,2176]{1,0:T(8,128)S(1)}, u32[]{:S(2)}, u32[]{:S(2)}) collective-permute-start(f32[8,2176]{1,0:T(8,128)S(1)} %constant_dynamic-update-slice_fusion), channel_id=1, source_target_pairs={{0,16},{8,24},{16,0},{24,8},{1,17},{9,25},{17,1},{25,9},{2,18},{10... | collective-permute-start | bytes 208904 | tf_op jit(solution)/shard_map/ppermute | solution.py:273
  6.6 4.3 %collective-permute-start = (f32[8,2176]{1,0:T(8,128)S(1)}, f32[8,2176]{1,0:T(8,128)S(1)}, u32[]{:S(2)}, u32[]{:S(2)}) collective-permute-start(f32[8,2176]{1,0:T(8,128)S(1)} %constant_dynamic-update-slice_fusion), channel_id=1, source_target_pairs={{0,8},{8,0},{16,24},{24,16},{1,9},{9,1},{17,25},{25,17},{2,10},{10... | collective-permute-start | bytes 208904 | tf_op jit(solution)/shard_map/ppermute | solution.py:273
  6.9 0.7 copy-start.5
  11.0 0.8 copy-start.2
  11.1 9.7 %copy-start = (f32[32,2048]{1,0:T(8,128)}, f32[32,2048]{1,0:T(8,128)S(1)}, u32[]{:S(2)}) copy-start(f32[32,2048]{1,0:T(8,128)S(1)} %slice_bitcast_fusion.right) | copy-start | bytes 786436
  11.9 8.9 %collective-permute-start.4 = (f32[4,4352]{1,0:T(4,128)S(1)}, f32[4,4352]{1,0:T(4,128)S(1)}, u32[]{:S(2)}, u32[]{:S(2)}) collective-permute-start(f32[4,4352]{1,0:T(4,128)S(1)} %pad_maximum_fusion.4), channel_id=1, source_target_pairs={{0,4},{1,5},{2,6},{3,7},{4,0},{5,1},{6,2},{7,3},{8,12},{9,13},{10,... | collective-permute-start | bytes 208904 | tf_op jit(solution)/shard_map/ppermute | solution.py:273
  14.5 6.2 %collective-permute-start.3 = (f32[4,4352]{1,0:T(4,128)S(1)}, f32[4,4352]{1,0:T(4,128)S(1)}, u32[]{:S(2)}, u32[]{:S(2)}) collective-permute-start(f32[4,4352]{1,0:T(4,128)S(1)} %pad_maximum_fusion.4), channel_id=1, source_target_pairs={{0,2},{1,3},{2,0},{3,1},{4,6},{5,7},{6,4},{7,5},{8,10},{9,11},{10,... | collective-permute-start | bytes 208904 | tf_op jit(solution)/shard_map/ppermute | solution.py:273
  16.1 6.2 %collective-permute-start.5 = (f32[4,4352]{1,0:T(4,128)S(1)}, f32[4,4352]{1,0:T(4,128)S(1)}, u32[]{:S(2)}, u32[]{:S(2)}) collective-permute-start(f32[4,4352]{1,0:T(4,128)S(1)} %pad_maximum_fusion.4), channel_id=1, source_target_pairs={{0,6},{1,7},{2,4},{3,5},{4,2},{5,3},{6,0},{7,1},{8,14},{9,15},{10,... | collective-permute-start | bytes 208904 | tf_op jit(solution)/shard_map/ppermute | solution.py:273
  16.3 8.7 %collective-permute-start.8 = (f32[32,128]{1,0:T(8,128)S(1)}, f32[32,128]{1,0:T(8,128)S(1)}, u32[]{:S(2)}, u32[]{:S(2)}) collective-permute-start(f32[32,128]{1,0:T(8,128)S(1)} %get-tuple-element.38), channel_id=1, source_target_pairs={{1,0},{2,1},{3,2},{4,3},{5,4},{6,5},{7,6},{9,8},{10,9},{11,10},{12... | collective-permute-start | bytes 49160 | tf_op jit(solution)/shard_map/ppermute | solution.py:281
  17.6 7.4 %collective-permute-start.7 = (f32[32,128]{1,0:T(8,128)S(1)}, f32[32,128]{1,0:T(8,128)S(1)}, u32[]{:S(2)}, u32[]{:S(2)}) collective-permute-start(f32[32,128]{1,0:T(8,128)S(1)} %get-tuple-element.39), channel_id=1, source_target_pairs={{0,1},{1,2},{2,3},{3,4},{4,5},{5,6},{6,7},{8,9},{9,10},{10,11},{11... | collective-permute-start | bytes 49160 | tf_op jit(solution)/shard_map/ppermute | solution.py:280
  22.3 1.6 %collective-permute-start.6 = (f32[4,4,4352]{2,1,0:T(4,128)S(1)}, f32[4,4,4352]{2,1,0:T(4,128)S(1)}, u32[]{:S(2)}, u32[]{:S(2)}) collective-permute-start(f32[4,4,4352]{2,1,0:T(4,128)S(1)} %bitcast_dynamic-update-slice_fusion.2), channel_id=1, source_target_pairs={{0,1},{1,0},{2,3},{3,2},{4,5},{5,4},{6,7},{7,6},{8,9},{9,8},{10,11... | collective-permute-start | bytes 835592 | tf_op jit(solution)/shard_map/ppermute | solution.py:273
  25.0 0.6 copy-start.3
  25.0 0.6 copy-start.4
  52.1 10.2 %collective-permute-start.9 = (f32[2,4,4,8192]{3,2,1,0:T(4,128)}, f32[2,4,4,8192]{3,2,1,0:T(4,128)S(1)}, u32[]{:S(2)}, u32[]{:S(2)}) collective-permute-start(f32[2,4,4,8192]{3,2,1,0:T(4,128)} %get-tuple-element.14), channel_id=1, source_target_pairs={{0,1},{1,0},{2,3},{3,2},{4,5},{5,4},{6,7},{7,6},{8,9},{9,8},{10,11... | collective-permute-start | bytes 3145736 | tf_op jit(solution)/shard_map/ppermute | solution.py:273
  63.8 6.3 %copy-start.1 = (f32[4,8,8192]{2,1,0:T(8,128)S(1)}, f32[4,8,8192]{2,1,0:T(8,128)}, u32[]{:S(2)}) copy-start(f32[4,8,8192]{2,1,0:T(8,128)} %get-tuple-element.17) | copy-start | bytes 3145732
  63.9 14.3 %collective-permute-start.10 = (f32[2,4,8192]{2,1,0:T(4,128)S(1)}, f32[2,4,8192]{2,1,0:T(4,128)S(1)}, u32[]{:S(2)}, u32[]{:S(2)}) collective-permute-start(f32[2,4,8192]{2,1,0:T(4,128)S(1)} %pad_maximum_fusion.1), channel_id=1, source_target_pairs={{0,2},{1,3},{2,0},{3,1},{4,6},{5,7},{6,4},{7,5},{8,10},{9,11},{10,... | collective-permute-start | bytes 786440 | tf_op jit(solution)/shard_map/ppermute | solution.py:273
  64.3 13.9 %collective-permute-start.11 = (f32[2,4,8192]{2,1,0:T(4,128)S(1)}, f32[2,4,8192]{2,1,0:T(4,128)S(1)}, u32[]{:S(2)}, u32[]{:S(2)}) collective-permute-start(f32[2,4,8192]{2,1,0:T(4,128)S(1)} %pad_maximum_fusion.2), channel_id=1, source_target_pairs={{0,4},{1,5},{2,6},{3,7},{4,0},{5,1},{6,2},{7,3},{8,12},{9,13},{10,... | collective-permute-start | bytes 786440 | tf_op jit(solution)/shard_map/ppermute | solution.py:273
  70.2 13.8 %collective-permute-start.12 = (f32[2,8,8192]{2,1,0:T(8,128)S(1)}, f32[2,8,8192]{2,1,0:T(8,128)S(1)}, u32[]{:S(2)}, u32[]{:S(2)}) collective-permute-start(f32[2,8,8192]{2,1,0:T(8,128)S(1)} %pad_maximum_fusion), channel_id=1, source_target_pairs={{0,8},{8,0},{16,24},{24,16},{1,9},{9,1},{17,25},{25,17},{2,10},{10... | collective-permute-start | bytes 1572872 | tf_op jit(solution)/shard_map/ppermute | solution.py:273
  84.0 8.2 %collective-permute-start.13 = (f32[1,4,8192]{2,1,0:T(4,128)S(1)}, f32[1,4,8192]{2,1,0:T(4,128)S(1)}, u32[]{:S(2)}, u32[]{:S(2)}) collective-permute-start(f32[1,4,8192]{2,1,0:T(4,128)S(1)} %bitcast.76), channel_id=1, source_target_pairs={{0,4},{1,5},{2,6},{3,7},{4,0},{5,1},{6,2},{7,3},{8,12},{9,13},{10,... | collective-permute-start | bytes 393224 | tf_op jit(solution)/shard_map/ppermute | solution.py:273
  85.2 7.0 %collective-permute-start.14 = (f32[1,4,8192]{2,1,0:T(4,128)S(1)}, f32[1,4,8192]{2,1,0:T(4,128)S(1)}, u32[]{:S(2)}, u32[]{:S(2)}) collective-permute-start(f32[1,4,8192]{2,1,0:T(4,128)S(1)} %bitcast.75), channel_id=1, source_target_pairs={{0,2},{1,3},{2,0},{3,1},{4,6},{5,7},{6,4},{7,5},{8,10},{9,11},{10,... | collective-permute-start | bytes 393224 | tf_op jit(solution)/shard_map/ppermute | solution.py:273
  86.7 9.8 %collective-permute-start.15 = (f32[1,8,8192]{2,1,0:T(8,128)S(1)}, f32[1,8,8192]{2,1,0:T(8,128)S(1)}, u32[]{:S(2)}, u32[]{:S(2)}) collective-permute-start(f32[1,8,8192]{2,1,0:T(8,128)S(1)} %bitcast.74), channel_id=1, source_target_pairs={{0,16},{8,24},{16,0},{24,8},{1,17},{9,25},{17,1},{25,9},{2,18},{10... | collective-permute-start | bytes 786440 | tf_op jit(solution)/shard_map/ppermute | solution.py:273
